TPU v7x, 32 devices: a whole 2x2x4 slice. The times are simulated.
32 devices in a mesh: rows: 16 (over z, y, x), cols: 2 (over core).
Axes of the slice: x: 2, y: 2, z: 4, core: 2. Of those that a mesh axis runs over, the one named last changes fastest.
Arguments:
- rhs: float32 [2, 96, 6144], P('cols', 'rows'), may hold values from -6 to 6
- pattern: int32 [48, 2], P(None, 'cols'), may hold values 0 or 1
- front_blocks: int32 [16, 4], replicated, may hold values from 0 to 47, as said below
- front_slot: int32 [16], replicated, may hold values from 0 to 31, as said below
- pivot_inverse: float32 [32, 256, 256], P('rows'), may hold values from -0.375 to 0.375
- update_factor: float32 [32, 256, 256], P('rows'), may hold values from -0.375 to 0.375
Outputs:
- solution: float32 [2, 96, 6144], P('cols', 'rows')
Inputs may be any that keep to these rules, and one draw needn't show every extreme that they name: `front_blocks`: columns 0 and 1 together name every row block that is no contribution block exactly once; columns 2 and 3 of a front are two different blocks, never a pivot block of any front. `front_slot`: all different; slot s belongs to index s // 2 of rows; some index holds 2 fronts in every draw; slots that no front names are unused.
All inputs are finite; a program needn't handle non-finite values. No bound on the sum of `pattern` on one device may be relied on, other than what follows from the above.
Results may differ from a plain program's by a relative error of at most 0.0001.
Values sent between devices are 32-bit elements; how exact they have to be, the bound alone decides.
A program may use at most 64 MiB of HBM per device.

v0:
```python
import jax
import jax.numpy as jnp
from jax import lax
from jax.sharding import PartitionSpec as P

BLOCK = 128
PIV = 256


def solve_slots(arrived, inverse_part, factor_part):
    width = inverse_part.shape[1]
    strict_lower = jnp.tril(jnp.ones((width, width), jnp.float32), -1)
    inverse = jnp.eye(width, dtype=jnp.float32)[None] + strict_lower[None] * inverse_part
    solved = jnp.einsum("kcj,kij->kci", arrived, inverse, precision=lax.Precision.HIGHEST)
    update = jnp.einsum("kcj,kij->kci", solved, factor_part, precision=lax.Precision.HIGHEST)
    return jnp.concatenate([solved, update], axis=2)


def on_device(rhs, pattern, front_blocks, front_slot, pivot_inverse, update_factor):
    fronts = front_blocks.shape[0]
    columns = rhs.shape[1]
    total_rows = rhs.shape[2]
    block_count = total_rows // BLOCK
    slot_dev = pivot_inverse.shape[0]
    devices = lax.axis_size("rows")
    pivot_blocks = front_blocks[:, :2].reshape(-1)
    contrib_blocks = front_blocks[:, 2:].reshape(-1)
    block_mask = pattern[:, 0].astype(jnp.float32)
    masked = rhs[0].reshape(columns, block_count, BLOCK) * block_mask[None, :, None]
    picked = jnp.swapaxes(
        jnp.take(masked, pivot_blocks, axis=1).reshape(columns, fronts, PIV), 0, 1
    )
    outbound = jnp.zeros((slot_dev * devices, columns, PIV), jnp.float32).at[front_slot].set(picked)
    arrived = lax.all_to_all(outbound, "rows", split_axis=0, concat_axis=1, tiled=True)
    worked = solve_slots(arrived, pivot_inverse, update_factor)
    returned = lax.all_to_all(worked, "rows", split_axis=1, concat_axis=0, tiled=True)
    gotten = returned[front_slot]
    solved = jnp.swapaxes(gotten[:, :, :PIV], 0, 1).reshape(columns, 2 * fronts, BLOCK)
    update = jnp.swapaxes(gotten[:, :, PIV:], 0, 1).reshape(columns, 2 * fronts, BLOCK)
    result = masked.at[:, pivot_blocks].set(solved)
    result = result.at[:, contrib_blocks].add(-update)
    return result.reshape(columns, total_rows)[None]


def solution(mesh):
    return jax.shard_map(
        on_device,
        mesh=mesh,
        in_specs=(
            P("cols", "rows", None),
            P(None, "cols"),
            P(),
            P(),
            P("rows", None, None),
            P("rows", None, None),
        ),
        out_specs=P("cols", "rows", None),
        check_vma=False,
    )
```

profile of v0, /device:TPU:0, one launch (start us, length us, event | category | flops | bytes accessed | tf_op | source)
XLA Modules:
  0.0 48.0 jit_solution(16247769093487404575)
XLA Ops:
  0.0 0.0 copy-start
  0.0 0.0 copy-start.2
  0.0 0.8 %fusion.10 = (s32[16,2]{0,1:T(2,128)S(1)}, s32[16,2]{0,1:T(2,128)S(1)}) fusion(s32[16,4]{0,1:T(4,128)} %param.8), kind=kLoop, calls=%fused_computation.31 | loop fusion | bytes 512 | tf_op jit(solution)/shard_map/slice | solution.py:27
  0.8 0.0 copy-done.2
  0.8 0.1 copy.33
  0.9 0.1 reshape.108
  1.0 0.0 copy-start.3
  1.0 0.6 %copy-done.3 = s32[48,1]{0,1:T(1,128)S(1)} copy-done((s32[48,1]{0,1:T(1,128)S(1)}, s32[48,1]{0,1:T(1,128)}, u32[]{:S(2)}) %copy-start.3) | copy-done | bytes 216
  1.7 0.1 copy.34
  1.8 0.1 broadcast_in_dim.35
  1.8 0.0 copy-start.4
  1.9 0.6 %copy-done.4 = s32[16]{0:T(128)S(1)} copy-done((s32[16]{0:T(128)S(1)}, s32[16]{0:T(128)}, u32[]{:S(2)}) %copy-start.4) | copy-done | bytes 88
  2.5 1.0 %copy_multiply_fusion = f32[6,48,128]{2,0,1:T(8,128)S(1)} fusion(f32[6,48,128]{2,1,0:T(8,128)} %bitcast.45, f32[48]{0:T(128)S(1)} %convert_bitcast_fusion), kind=kLoop, calls=%fused_computation.16 | loop fusion | flops 36864 | bytes 295104 | tf_op jit(solution)/shard_map/mul | solution.py:29
  3.5 0.6 %gather_fusion = f32[32,6,128]{2,1,0:T(8,128)S(1)} fusion(f32[6,48,128]{2,0,1:T(8,128)S(1)} %copy_multiply_fusion, s32[1024]{0:T(1024)S(1)} %pad_clamp_fusion.1), kind=kCustom, calls=%fused_computation | custom fusion | bytes 196736 | tf_op jit(solution)/shard_map/jit(_take)/gather | solution.py:31
  4.2 0.7 %broadcast_in_dim.33 = f32[32,6,256]{2,1,0:T(8,128)} broadcast(f32[]{:T(128)} %constant.10.clone.1), dimensions={} | broadcast | bytes 196612 | tf_op jit(solution)/shard_map/broadcast_in_dim | solution.py:33
  4.9 2.2 %scatter_fusion = f32[32,6,256]{2,1,0:T(8,128)} fusion(f32[32,6,256]{2,1,0:T(8,128)} %broadcast_in_dim.33, s32[16]{0:T(128)S(1)} %compare_select_fusion.2, f32[16,6,256]{2,1,0:T(8,128)S(1)} %select_bitcast_fusion), kind=kCustom, calls=%fused_computation.2 | custom fusion | bytes 294976 | tf_op jit(solution)/shard_map/scatter | solution.py:33
  7.1 8.3 %all-to-all-start = ((f32[32,6,256]{2,1,0:T(8,128)}), f32[32,6,256]{2,1,0:T(8,128)S(1)}, u32[]{:S(2)}, u32[]{:S(2)}) async-start(f32[32,6,256]{2,1,0:T(8,128)} %scatter_fusion), calls=%async_computation | async-start | bytes 524288 | tf_op jit(solution)/shard_map/all_to_all | solution.py:34
  15.4 0.0 copy-start.1
  15.5 0.1 fusion.6
  15.6 9.7 %all-to-all-done = f32[32,6,256]{2,1,0:T(8,128)S(1)} async-done(((f32[32,6,256]{2,1,0:T(8,128)}), f32[32,6,256]{2,1,0:T(8,128)S(1)}, u32[]{:S(2)}, u32[]{:S(2)}) %all-to-all-start) | async-done | bytes 196640 | tf_op jit(solution)/shard_map/all_to_all | solution.py:34
  25.3 0.1 copy.35
  25.4 0.0 copy-done.1
  25.4 0.6 %fusion = f32[2,96,256]{2,1,0:T(8,128)S(1)} fusion(f32[2,256,256]{2,1,0:T(8,128)S(1)} %copy-done.1, f32[256,256]{1,0:T(8,128)S(1)} %fusion.6, f32[256,256]{1,0:T(8,128)S(1)} %fusion.5, f32[2,96,256]{2,0,1:T(2,128)S(1)} %bitcast.41), kind=kOutput, calls=%fused_computation.5 | convolution fusion | flops 151257088 | bytes 1441792 | tf_op jit(solution)/shard_map/kcj,kij->kci/dot_general | solution.py:14
  26.1 0.0 copy-done
  26.1 0.6 %fusion.11 = f32[2,96,256]{2,1,0:T(8,128)S(1)} fusion(f32[2,96,256]{2,1,0:T(8,128)S(1)} %fusion, f32[2,256,256]{2,1,0:T(8,128)S(1)} %copy-done), kind=kOutput, calls=%fused_computation.32 | convolution fusion | flops 150994944 | bytes 917504 | tf_op jit(solution)/shard_map/kcj,kij->kci/dot_general | solution.py:15
  26.7 1.1 %copy.37 = f32[2,96,512]{2,0,1:T(2,128)} copy(f32[2,96,512]{2,1,0:T(8,128)S(1)} %pad_maximum_fusion) | data formatting | bytes 786432 | tf_op jit(solution)/shard_map/concatenate | solution.py:16
  27.8 3.6 %all-to-all-start.1 = ((f32[2,96,512]{2,0,1:T(2,128)}), f32[2,96,512]{2,0,1:T(2,128)S(1)}, u32[]{:S(2)}, u32[]{:S(2)}) async-start(f32[2,96,512]{2,0,1:T(2,128)} %copy.37), calls=%async_computation.1 | async-start | bytes 786432 | tf_op jit(solution)/shard_map/all_to_all | solution.py:36
  31.3 0.1 copy.40
  31.4 0.1 reshape.110
  31.5 11.8 %all-to-all-done.1 = f32[2,96,512]{2,0,1:T(2,128)S(1)} async-done(((f32[2,96,512]{2,0,1:T(2,128)}), f32[2,96,512]{2,0,1:T(2,128)S(1)}, u32[]{:S(2)}, u32[]{:S(2)}) %all-to-all-start.1) | async-done | bytes 393248 | tf_op jit(solution)/shard_map/all_to_all | solution.py:36
  43.3 0.1 copy.42
  43.4 0.6 %gather_fusion.1 = f32[16,6,512]{2,1,0:T(8,128)S(1)} fusion(f32[32,6,512]{2,1,0:T(8,128)S(1)} %bitcast.39, s32[1024]{0:T(1024)S(1)} %pad_clamp_fusion), kind=kCustom, calls=%fused_computation.1 | custom fusion | bytes 393280 | tf_op jit(solution)/shard_map/gather | solution.py:37
  44.0 1.5 %scatter_fusion.1 = f32[6,48,128]{2,0,1:T(8,128)S(1)} fusion(f32[6,48,128]{2,0,1:T(8,128)S(1)} %copy_multiply_fusion, s32[32]{0:T(128)S(1)} %fusion.8, f32[32,6,128]{2,1,0:T(8,128)S(1)} %bitcast.44), kind=kCustom, calls=%fused_computation.3 | custom fusion | bytes 295040 | tf_op jit(solution)/shard_map/scatter | solution.py:40
  45.5 1.7 %scatter_fusion.2 = f32[6,48,128]{2,0,1:T(8,128)S(1)} fusion(f32[6,48,128]{2,0,1:T(8,128)S(1)} %scatter_fusion.1, s32[32]{0:T(128)S(1)} %fusion.9, f32[32,6,128]{2,1,0:T(8,128)S(1)} %bitcast.43), kind=kCustom, calls=%fused_computation.4 | custom fusion | flops 24576 | bytes 295040 | tf_op jit(solution)/shard_map/scatter-add | solution.py:41
  47.2 0.8 %copy.41 = f32[1,6,6144]{2,0,1:T(1,128)} copy(f32[1,6,6144]{2,1,0:T(8,128)S(1)} %bitcast.37) | data formatting | bytes 294912 | tf_op jit(solution)/shard_map/broadcast_in_dim;reshape | solution.py:42
  (13 shorter events, 0.1 us)
Async XLA Ops:
  0.0 26.1 %copy-start = (f32[2,256,256]{2,1,0:T(8,128)S(1)}, f32[2,256,256]{2,1,0:T(8,128)}, u32[]{:S(2)}) copy-start(f32[2,256,256]{2,1,0:T(8,128)} %param.11) | copy-start | bytes 1572868
  0.0 0.8 %copy-start.2 = (s32[16,4]{0,1:T(4,128)S(1)}, s32[16,4]{0,1:T(4,128)}, u32[]{:S(2)}) copy-start(s32[16,4]{0,1:T(4,128)} %param.8) | copy-start | bytes 772
  1.0 0.7 %copy-start.3 = (s32[48,1]{0,1:T(1,128)S(1)}, s32[48,1]{0,1:T(1,128)}, u32[]{:S(2)}) copy-start(s32[48,1]{0,1:T(1,128)} %param.7) | copy-start | bytes 580
  1.8 0.7 %copy-start.4 = (s32[16]{0:T(128)S(1)}, s32[16]{0:T(128)}, u32[]{:S(2)}) copy-start(s32[16]{0:T(128)} %param.9) | copy-start | bytes 196
  7.1 18.2 %all-to-all-start = ((f32[32,6,256]{2,1,0:T(8,128)}), f32[32,6,256]{2,1,0:T(8,128)S(1)}, u32[]{:S(2)}, u32[]{:S(2)}) async-start(f32[32,6,256]{2,1,0:T(8,128)} %scatter_fusion), calls=%async_computation | async-start | bytes 524288 | tf_op jit(solution)/shard_map/all_to_all | solution.py:34
  15.4 10.0 %copy-start.1 = (f32[2,256,256]{2,1,0:T(8,128)S(1)}, f32[2,256,256]{2,1,0:T(8,128)}, u32[]{:S(2)}) copy-start(f32[2,256,256]{2,1,0:T(8,128)} %param.10) | copy-start | bytes 1572868
  27.8 15.5 %all-to-all-start.1 = ((f32[2,96,512]{2,0,1:T(2,128)}), f32[2,96,512]{2,0,1:T(2,128)S(1)}, u32[]{:S(2)}, u32[]{:S(2)}) async-start(f32[2,96,512]{2,0,1:T(2,128)} %copy.37), calls=%async_computation.1 | async-start | bytes 786432 | tf_op jit(solution)/shard_map/all_to_all | solution.py:36
where the time goes:
time: 48.4 us; the launch traced here: 48 us
  waiting for transfers between devices  21.5 us (44%)
  starting transfers between devices  11.9 us (25%)
  local copies, waits for them, and re-layouts  10.2 us (21%)
  other arithmetic  2.92 us (6%)
  matrix products  1.25 us (3%)
    all_to_all x1, waiting for transfers between devices, on_device(): lax.all_to_all(worked, 'rows', split_axis=1, concat_axis=0, tiled=True)  11.8 us
    all_to_all x1, waiting for transfers between devices, on_device(): lax.all_to_all(outbound, 'rows', split_axis=0, concat_axis=1, tiled=True)  9.71 us
    all_to_all x1, starting transfers between devices, on_device(): lax.all_to_all(outbound, 'rows', split_axis=0, concat_axis=1, tiled=True)  8.34 us
    all_to_all x1, starting transfers between devices, on_device(): lax.all_to_all(worked, 'rows', split_axis=1, concat_axis=0, tiled=True)  3.56 us
    scatter x1, local copies, waits for them, and re-layouts, on_device(): jnp.zeros((slot_dev * devices, columns, PIV), jnp.float32).at[front_slot]  2.2 us
    scatter-add x1, other arithmetic, on_device(): result = result.at[:, contrib_blocks].add(-update)  1.65 us
    scatter x1, local copies, waits for them, and re-layouts, on_device(): result = masked.at[:, pivot_blocks].set(solved)  1.48 us
    unnamed x11, local copies, waits for them, and re-layouts  1.3 us
  transfers between devices with their start and end apart: 2, of which 2 were waited for; matrix products, arithmetic and copies ran while one was open for 1% of the time, Pallas kernels for 0%

commit v1 on v0

v1 whole, which is shorter than its diff:
```python
import functools

import jax
import jax.numpy as jnp
from jax import lax
from jax.experimental import pallas as pl
from jax.experimental.pallas import tpu as pltpu
from jax.sharding import PartitionSpec as P

BLOCK = 128
COLS = 6
PAIR = 2


def split(value):
    high = value.astype(jnp.bfloat16)
    low = (value - high.astype(jnp.float32)).astype(jnp.bfloat16)
    return high, low


def times_transposed(x, high, low):
    dims = (((1,), (1,)), ((), ()))
    x_high, x_low = split(x)
    dot = functools.partial(lax.dot_general, dimension_numbers=dims, preferred_element_type=jnp.float32)
    return dot(x_high, high) + (dot(x_low, high) + dot(x_high, low))


def kernel(
    n, fronts, blocks,
    rhs_hbm, pattern_hbm, fb_hbm, slot_hbm, inv_hbm, upd_hbm,
    out_ref,
    x, snd, rcv, back, pool, last, fourth, inv, upd, wide, coef,
    pattern, fb, slot, front_of, src, sep,
    local_sem, out_send, out_recv, back_send, back_recv,
):
    me = lax.axis_index("rows")
    col = lax.axis_index("cols")
    slots = PAIR * n
    seps = blocks - 2 * fronts

    def target(peer):
        return {"rows": peer, "cols": col}

    pieces = [
        (rhs_hbm, x), (pattern_hbm, pattern), (fb_hbm, fb), (slot_hbm, slot), (inv_hbm, inv), (upd_hbm, upd),
    ]
    loads = [pltpu.make_async_copy(a, b, local_sem.at[i]) for i, (a, b) in enumerate(pieces)]
    for load in (loads[1], loads[2], loads[3], loads[0], loads[4], loads[5]):
        load.start()

    barrier = pltpu.get_barrier_semaphore()

    def greet(i, carry):
        pl.semaphore_signal(
            barrier, inc=1, device_id=target(lax.rem(me + i, n)), device_id_type=pl.DeviceIdType.MESH
        )
        return carry

    lax.fori_loop(1, n, greet, 0)

    few = fronts <= 16

    def total(count, term):
        if few:
            values = [term(i) for i in range(count)]
            while len(values) > 1:
                pairs = [a + b for a, b in zip(values[::2], values[1::2])]
                values = pairs + ([values[-1]] if len(values) % 2 else [])
            return values[0]
        return lax.fori_loop(0, count, lambda i, t: t + term(i), 0)

    for load in loads[1:4]:
        load.wait()

    def find_front(s, carry):
        front_of[s] = jnp.minimum(total(fronts, lambda f: jnp.where(slot[f] == s, f, 0)), fronts - 1)
        return carry

    lax.fori_loop(0, slots, find_front, 0)
    loads[0].wait()

    def block_rows(b, first, count):
        mask = pattern[b].astype(jnp.float32)
        return x[pl.ds(first * blocks + b, count, stride=blocks), :] * mask

    def pack(d, carry):
        f0 = front_of[PAIR * d]
        f1 = front_of[PAIR * d + 1]
        snd[d, 0, 0:6, :] = block_rows(fb[0, f0], 0, COLS)
        snd[d, 1, 0:6, :] = block_rows(fb[1, f0], 0, COLS)
        snd[d, 2, 0:6, :] = block_rows(fb[0, f1], 0, COLS)
        b3 = fb[1, f1]
        for t in range(3):
            snd[d, t, 6:8, :] = block_rows(b3, 2 * t, 2)
        return carry

    lax.fori_loop(0, n, pack, 0)
    pl.semaphore_wait(barrier, n - 1)

    order = sorted(range(1, n), key=lambda i: abs(i - n // 2))
    runs = order if n <= 16 else None

    def for_peers(body):
        if runs is not None:
            for i in runs:
                body(lax.rem(me + i, n))
        else:
            def step(i, carry):
                body(lax.rem(me + i, n))
                return carry
            lax.fori_loop(1, n, step, 0)

    def send_out(peer):
        pltpu.make_async_remote_copy(
            src_ref=snd.at[peer], dst_ref=rcv.at[me], send_sem=out_send, recv_sem=out_recv,
            device_id=target(peer), device_id_type=pl.DeviceIdType.MESH,
        ).start()

    for_peers(send_out)
    rcv[pl.ds(me, 1)] = snd[pl.ds(me, 1)]

    loads[4].wait()
    loads[5].wait()
    width = inv.shape[1]
    strict = lax.broadcasted_iota(jnp.int32, (width, width), 0) > lax.broadcasted_iota(jnp.int32, (width, width), 1)
    for k in range(PAIR):
        wide[k, 0], wide[k, 1] = split(jnp.where(strict, inv[k], 0.0))
        wide[k, 2], wide[k, 3] = split(upd[k])

    def find_source(b, rank):
        def term(e):
            h, f = e // fronts, e % fronts
            return jnp.where(fb[h, f] == b, 3 * slot[f] + h + 1, 0)

        place = total(2 * fronts, term)
        is_sep = place == 0
        src[b] = jnp.minimum(jnp.where(is_sep, 3 * slots + rank, place - 1), 3 * slots + seps - 1)
        return rank + jnp.where(is_sep, 1, 0)

    lax.fori_loop(0, blocks, find_source, 0)

    def find_separator(j, carry):
        def step(b, t):
            return t + jnp.where(src[b] == 3 * slots + j, b, 0)
        b = lax.fori_loop(0, blocks, step, 0, unroll=8)
        b = jnp.minimum(b, blocks - 1)
        sep[j] = b

        def weight(e, c):
            h, f = e // fronts, e % fronts
            hit = jnp.where(fb[2 + h, f] == b, -1.0, 0.0).astype(jnp.float32)
            coef[pl.ds(j * 2 * fronts + e, 1), :] = jnp.full((1, BLOCK), hit, jnp.float32)
            return c
        lax.fori_loop(0, 2 * fronts, weight, 0, unroll=8)
        return carry

    lax.fori_loop(0, seps, find_separator, 0)

    def landed(buffer, count, sem):
        view = buffer.at[pl.ds(0, count)]
        return pltpu.make_async_copy(view, view, sem)

    landed(rcv, n - 1, out_recv).wait()

    fourth[:, 6:8, :] = jnp.zeros((n, 2, BLOCK), jnp.float32)
    for t in range(3):
        fourth[:, 2 * t:2 * t + 2, :] = rcv[:, t, 6:8, :]

    def flat(a):
        return a.reshape(8 * n, BLOCK)

    for k in range(PAIR):
        if k == 0:
            pivots = jnp.concatenate([flat(rcv[:, 0]), flat(rcv[:, 1])], axis=1)
        else:
            pivots = jnp.concatenate([flat(rcv[:, 2]), flat(fourth[...])], axis=1)
        solved = pivots + times_transposed(pivots, wide[k, 0], wide[k, 1])
        update = times_transposed(solved, wide[k, 2], wide[k, 3])
        quads = [
            half.reshape(n, 8, BLOCK)
            for half in (solved[:, :BLOCK], solved[:, BLOCK:], update[:, :BLOCK], update[:, BLOCK:])
        ]
        for t in range(3):
            back[k, :, t, 0:6, :] = quads[t][:, 0:6]
            back[k, :, t, 6:8, :] = quads[3][:, 2 * t:2 * t + 2]

        def send_back(peer, k=k):
            pltpu.make_async_remote_copy(
                src_ref=back.at[k, peer], dst_ref=pool.at[pl.ds(3 * (PAIR * me + k), 3)],
                send_sem=back_send, recv_sem=back_recv,
                device_id=target(peer), device_id_type=pl.DeviceIdType.MESH,
            ).start()

        for_peers(send_back)
        pool[pl.ds(3 * (PAIR * me + k), 3)] = back[k, me]

    landed(pool, 3 * PAIR * (n - 1), back_recv).wait()

    for t in range(3):
        last[:, 2 * t:2 * t + 2, :] = pool[pl.ds(t, slots, stride=3), 6:8, :]

    def add_up(j, carry):
        b = sep[j]
        acc = block_rows(b, 0, COLS)

        def term_first(f, a):
            return a + coef[pl.ds(j * 2 * fronts + f, 1), :] * pool[3 * slot[f] + 2, 0:6, :]

        def term_second(f, a):
            return a + coef[pl.ds(j * 2 * fronts + fronts + f, 1), :] * last[slot[f]]
        acc = lax.fori_loop(0, fronts, term_first, acc, unroll=8)
        acc = lax.fori_loop(0, fronts, term_second, acc, unroll=8)
        pool[3 * slots + j, 0:6, :] = acc
        return carry

    lax.fori_loop(0, seps, add_up, 0)

    def place(b, carry):
        out_ref[pl.ds(b, COLS, stride=blocks), :] = pool[src[b], 0:6, :]
        return carry

    lax.fori_loop(0, blocks, place, 0, unroll=8)

    landed(snd, n - 1, out_send).wait()
    for k in range(PAIR):
        landed(back.at[k], n - 1, back_send).wait()


def on_device(n, rhs, pattern, front_blocks, front_slot, pivot_inverse, update_factor):
    fronts = front_blocks.shape[0]
    columns, total_rows = rhs.shape[1:]
    blocks = total_rows // BLOCK
    assert columns == COLS and pivot_inverse.shape[0] == PAIR
    width = pivot_inverse.shape[1]
    slots = PAIR * n
    seps = blocks - 2 * fronts
    f32, i32 = jnp.float32, jnp.int32
    result = pl.pallas_call(
        functools.partial(kernel, n, fronts, blocks),
        out_shape=jax.ShapeDtypeStruct((columns * blocks, BLOCK), f32),
        in_specs=[pl.BlockSpec(memory_space=pl.ANY)] * 6,
        out_specs=pl.BlockSpec(memory_space=pltpu.VMEM),
        scratch_shapes=[
            pltpu.VMEM((columns * blocks, BLOCK), f32),
            pltpu.VMEM((n, 3, 8, BLOCK), f32),
            pltpu.VMEM((n, 3, 8, BLOCK), f32),
            pltpu.VMEM((PAIR, n, 3, 8, BLOCK), f32),
            pltpu.VMEM((3 * slots + seps, 8, BLOCK), f32),
            pltpu.VMEM((slots, 6, BLOCK), f32),
            pltpu.VMEM((n, 8, BLOCK), f32),
            pltpu.VMEM((PAIR, width, width), f32),
            pltpu.VMEM((PAIR, width, width), f32),
            pltpu.VMEM((PAIR, 4, width, width), jnp.bfloat16),
            pltpu.VMEM((seps * 2 * fronts, BLOCK), f32),
            pltpu.SMEM((blocks,), i32),
            pltpu.SMEM((4, fronts), i32),
            pltpu.SMEM((fronts,), i32),
            pltpu.SMEM((slots,), i32),
            pltpu.SMEM((blocks,), i32),
            pltpu.SMEM((seps,), i32),
            pltpu.SemaphoreType.DMA((6,)),
            pltpu.SemaphoreType.DMA,
            pltpu.SemaphoreType.DMA,
            pltpu.SemaphoreType.DMA,
            pltpu.SemaphoreType.DMA,
        ],
        compiler_params=pltpu.CompilerParams(collective_id=0, has_side_effects=True),
    )(
        rhs.reshape(columns * blocks, BLOCK),
        pattern.reshape(-1),
        front_blocks.T,
        front_slot,
        pivot_inverse,
        update_factor,
    )
    return result.reshape(1, columns, total_rows)


def solution(mesh):
    return jax.shard_map(
        functools.partial(on_device, mesh.shape["rows"]),
        mesh=mesh,
        in_specs=(
            P("cols", "rows", None),
            P(None, "cols"),
            P(),
            P(),
            P("rows", None, None),
            P("rows", None, None),
        ),
        out_specs=P("cols", "rows", None),
        check_vma=False,
    )
```

time: 48.4 us -> 30.8 us (0.64)
  Pallas kernels: 0 us -> 29.1 us
  waiting for transfers between devices: 21.5 us -> 0 us
  starting transfers between devices: 11.9 us -> 0 us
  local copies, waits for them, and re-layouts: 10.2 us -> 1.58 us
  other arithmetic: 2.92 us -> 0 us
  matrix products: 1.25 us -> 0 us
    pallas_call x0 -> x1, Pallas kernels: none -> 29.1 us  [on_device(): pl.pallas_call(functools.partial(kernel, n, fronts, blocks), out_shape=ja...]
    all_to_all x2 -> x0, waiting for transfers between devices: 21.5 us -> none  [the longest x1 11.8 us: on_device(): lax.all_to_all(worked, 'rows', split_axis=1, concat_axis=0, tiled=True)]
    all_to_all x2 -> x0, starting transfers between devices: 11.9 us -> none  [the longest x1 8.34 us: on_device(): lax.all_to_all(outbound, 'rows', split_axis=0, concat_axis=1, tiled=True)]
    scatter x2 -> x0, local copies, waits for them, and re-layouts: 3.69 us -> none  [the longest x1 2.2 us: on_device(): jnp.zeros((slot_dev * devices, columns, PIV), jnp.float32).at[front_slot]]
    scatter-add x1 -> x0, other arithmetic: 1.65 us -> none  [on_device(): result = result.at[:, contrib_blocks].add(-update)]
    dot_general x2 -> x0, matrix products: 1.25 us -> none  [the longest x1 0.64 us: solve_slots(): jnp.einsum('kcj,kij->kci', arrived, inverse, precision=lax.Precision.HIGH...]
    gather x2 -> x0, local copies, waits for them, and re-layouts: 1.15 us -> none  [the longest x1 0.59 us: on_device(): jnp.take(masked, pivot_blocks, axis=1).reshape(columns, fronts, PIV)]
    concatenate x1 -> x0, local copies, waits for them, and re-layouts: 1.06 us -> none  [solve_slots(): return jnp.concatenate([solved, update], axis=2)]
  transfers between devices with their start and end apart: 2 -> 0, of which waited for: 2 -> 0; matrix products, arithmetic and copies ran while one was open for 1% -> 0% of each run, Pallas kernels for 0% -> 0%
where the time goes in v1:
time: 30.8 us; the launch traced here: 30.7 us
  Pallas kernels  29.1 us (94%)
  local copies, waits for them, and re-layouts  1.58 us (5%)
    pallas_call x1, Pallas kernels, on_device(): pl.pallas_call(functools.partial(kernel, n, fronts, blocks), out_shape=ja...  29.1 us
    unnamed x1, local copies, waits for them, and re-layouts  1.58 us

profile of v1, /device:TPU:0, one launch (start us, length us, event | category | flops | bytes accessed | tf_op | source)
XLA Modules:
  0.0 30.7 jit_solution(12653507931737116064)
XLA Ops:
  0.0 29.1 %shard_map.64 = f32[288,128]{1,0:T(8,128)} custom-call(f32[288,128]{1,0:T(8,128)} %bitcast.5, s32[48]{0:T(128)} %bitcast.7, s32[4,16]{1,0:T(4,128)} %bitcast.6, s32[16]{0:T(128)} %slot_hbm.1, f32[2,256,256]{2,1,0:T(8,128)} %inv_hbm.1, f32[2,256,256]{2,1,0:T(8,128)} %upd_hbm.1), custom_call_target="tpu_custom_call" | custom-call | tf_op jit(solution)/shard_map/pallas_call | solution.py:238
  29.1 1.6 %copy.10 = f32[1,6,6144]{2,0,1:T(1,128)} copy(f32[1,6,6144]{2,0,1:T(1,128)} %bitcast.4) | data formatting | bytes 294912

commit v2 on v1

v2 whole, which is shorter than its diff:
```python
import functools

import jax
import jax.numpy as jnp
from jax import lax
from jax.experimental import pallas as pl
from jax.experimental.pallas import tpu as pltpu
from jax.sharding import PartitionSpec as P

BLOCK = 128
COLS = 6
PAIR = 2


def split(value):
    high = value.astype(jnp.bfloat16)
    low = (value - high.astype(jnp.float32)).astype(jnp.bfloat16)
    return high, low


def times_transposed(x, high, low):
    dims = (((1,), (1,)), ((), ()))
    x_high, x_low = split(x)
    dot = functools.partial(lax.dot_general, dimension_numbers=dims, preferred_element_type=jnp.float32)
    return dot(x_high, high) + (dot(x_low, high) + dot(x_high, low))


def kernel(
    n, fronts, blocks, chunk,
    rhs_hbm, pattern_hbm, fb_hbm, slot_hbm, inv_hbm, upd_hbm,
    out_ref,
    x, snd, rcv, back, pool, last, halves, inv, upd, wide, sep_rows, coef,
    pattern, fb, slot, front_of, place_of, src, sep,
    local_sem, out_send, out_recv, back_send, back_recv,
):
    me = lax.axis_index("rows")
    col = lax.axis_index("cols")
    slots = PAIR * n
    seps = blocks - 2 * fronts
    few = n <= 16

    def target(peer):
        return {"rows": peer, "cols": col}

    order = sorted(range(1, n), key=lambda i: abs(i - n // 2))

    def for_peers(body):
        if few:
            for i in order:
                body(lax.rem(me + i, n))
        else:
            def step(i, carry):
                body(lax.rem(me + i, n))
                return carry
            lax.fori_loop(1, n, step, 0)

    def repeat(count, body, unroll=1):
        def step(i, carry):
            body(i)
            return carry
        lax.fori_loop(0, count, step, 0, unroll=unroll if few else 1)

    pieces = [
        (rhs_hbm, x), (pattern_hbm, pattern), (fb_hbm, fb), (slot_hbm, slot), (inv_hbm, inv), (upd_hbm, upd),
    ]
    loads = [pltpu.make_async_copy(a, b, local_sem.at[i]) for i, (a, b) in enumerate(pieces)]
    for i in (3, 2, 1, 0, 4, 5):
        loads[i].start()

    barrier = pltpu.get_barrier_semaphore()
    for_peers(lambda peer: pl.semaphore_signal(
        barrier, inc=1, device_id=target(peer), device_id_type=pl.DeviceIdType.MESH
    ))

    def total(count, term):
        if few:
            values = [term(i) for i in range(count)]
            while len(values) > 1:
                pairs = [a + b for a, b in zip(values[::2], values[1::2])]
                values = pairs + ([values[-1]] if len(values) % 2 else [])
            return values[0]
        return lax.fori_loop(0, count, lambda i, t: t + term(i), 0)

    loads[3].wait()

    def find_front(s):
        front_of[s] = jnp.minimum(total(fronts, lambda f: jnp.where(slot[f] == s, f, 0)), fronts - 1)

    repeat(slots, find_front, 2)
    for i in (2, 1, 0):
        loads[i].wait()

    def block_rows(b, first, count):
        mask = pattern[b].astype(jnp.float32)
        return x[pl.ds(first * blocks + b, count, stride=blocks), :] * mask

    def pack(d):
        for k in range(PAIR):
            f = front_of[PAIR * d + k]
            b0, b1 = fb[0, f], fb[1, f]
            snd[k, d, 0] = block_rows(b0, 0, 4)
            snd[k, d, 1, 0:2, :] = block_rows(b0, 4, 2)
            snd[k, d, 1, 2:4, :] = block_rows(b1, 0, 2)
            snd[k, d, 2] = block_rows(b1, 2, 4)

    repeat(n, pack, 2)
    pl.semaphore_wait(barrier, n - 1)

    for k in range(PAIR):
        for_peers(lambda peer, k=k: pltpu.make_async_remote_copy(
            src_ref=snd.at[k, peer], dst_ref=rcv.at[k, me], send_sem=out_send.at[k], recv_sem=out_recv.at[k],
            device_id=target(peer), device_id_type=pl.DeviceIdType.MESH,
        ).start())
        rcv[k, me] = snd[k, me]

    loads[4].wait()
    loads[5].wait()
    width = inv.shape[1]
    strict = lax.broadcasted_iota(jnp.int32, (width, width), 0) > lax.broadcasted_iota(jnp.int32, (width, width), 1)
    for k in range(PAIR):
        wide[k, 0], wide[k, 1] = split(jnp.where(strict, inv[k], 0.0))
        wide[k, 2], wide[k, 3] = split(upd[k])
    halves[...] = jnp.zeros(halves.shape, jnp.float32)
    last[...] = jnp.zeros(last.shape, jnp.float32)

    def find_place(f):
        s = slot[f]
        place_of[f] = 3 * (lax.rem(s, PAIR) * n + lax.div(s, PAIR)) + 1

    repeat(fronts, find_place, 4)

    def find_source(b, rank):
        def term(f):
            at = place_of[f]
            return jnp.where(fb[0, f] == b, at, 0) + jnp.where(fb[1, f] == b, at + 1, 0)

        place = total(fronts, term)
        is_sep = place == 0
        src[b] = jnp.minimum(jnp.where(is_sep, 3 * slots + rank, place - 1), 3 * slots + seps - 1)
        return rank + jnp.where(is_sep, 1, 0)

    lax.fori_loop(0, blocks, find_source, 0)

    def landed(buffer, count, sem):
        view = buffer.at[pl.ds(0, count)]
        return pltpu.make_async_copy(view, view, sem)

    def flat(a):
        return a.reshape(8 * n, BLOCK)

    for k in range(PAIR):
        landed(rcv.at[k], n - 1, out_recv.at[k]).wait()
        halves[0, :, 0:4, :] = rcv[k, :, 0]
        halves[0, :, 4:6, :] = rcv[k, :, 1, 0:2, :]
        halves[1, :, 0:2, :] = rcv[k, :, 1, 2:4, :]
        halves[1, :, 2:6, :] = rcv[k, :, 2]
        pivots = jnp.concatenate([flat(halves[0]), flat(halves[1])], axis=1)
        solved = pivots + times_transposed(pivots, wide[k, 0], wide[k, 1])
        update = times_transposed(solved, wide[k, 2], wide[k, 3])
        quads = [
            half.reshape(n, 8, BLOCK)
            for half in (solved[:, :BLOCK], solved[:, BLOCK:], update[:, :BLOCK], update[:, BLOCK:])
        ]
        for t in range(3):
            back[k, :, t, 0:6, :] = quads[t][:, 0:6]
            back[k, :, t, 6:8, :] = quads[3][:, 2 * t:2 * t + 2]

        for_peers(lambda peer, k=k: pltpu.make_async_remote_copy(
            src_ref=back.at[k, peer], dst_ref=pool.at[pl.ds(3 * (k * n + me), 3)],
            send_sem=back_send.at[k], recv_sem=back_recv.at[k],
            device_id=target(peer), device_id_type=pl.DeviceIdType.MESH,
        ).start())
        pool[pl.ds(3 * (k * n + me), 3)] = back[k, me]

    def find_separator(j):
        b = lax.fori_loop(
            0, blocks, lambda b, t: t + jnp.where(src[b] == 3 * slots + j, b, 0), 0, unroll=16 if few else 1
        )
        b = jnp.minimum(b, blocks - 1)
        sep[j] = b
        sep_rows[pl.ds(j, 1), :] = jnp.full((1, BLOCK), b, jnp.int32)
        pool[3 * slots + j, 0:6, :] = block_rows(b, 0, COLS)
        pool[3 * slots + j, 6:8, :] = jnp.zeros((2, BLOCK), jnp.float32)

    repeat(seps, find_separator)

    def weigh(g):
        rows = sep_rows[pl.ds(pl.multiple_of(g * chunk, chunk), chunk), :]

        def one_slot(s):
            f = front_of[s]
            used = slot[f] == s
            q = lax.rem(s, PAIR) * n + lax.div(s, PAIR)
            for h in range(2):
                named = jnp.where(used, fb[2 + h, f], -1)
                coef[(g * slots + q) * 2 + h] = jnp.where(rows == named, -1.0, 0.0)

        repeat(slots, one_slot, 4)

    repeat(seps // chunk, weigh)

    for k in range(PAIR):
        landed(pool, 3 * (n - 1), back_recv.at[k]).wait()
        for t in range(3):
            last[k * n:(k + 1) * n, 2 * t:2 * t + 2, :] = pool[pl.ds(3 * k * n + t, n, stride=3), 6:8, :]

        def add_up(g, k=k):
            first = 3 * slots + g * chunk

            def one_slot(o, accs):
                q = k * n + o
                parts = (pool[3 * q + 2], last[q])
                for h in range(2):
                    row = (g * slots + q) * 2 + h
                    accs = tuple(a + coef[row, j:j + 1, :] * parts[h] for j, a in enumerate(accs))
                return accs

            accs = tuple(pool[first + j] for j in range(chunk))
            accs = lax.fori_loop(0, n, one_slot, accs, unroll=4 if few else 1)
            for j in range(chunk):
                pool[first + j] = accs[j]

        repeat(seps // chunk, add_up)

    def put(b):
        out_ref[pl.ds(b, COLS, stride=blocks), :] = pool[src[b], 0:6, :]

    repeat(blocks, put, 16)

    for k in range(PAIR):
        landed(snd.at[k], n - 1, out_send.at[k]).wait()
        landed(back.at[k], n - 1, back_send.at[k]).wait()


def on_device(n, rhs, pattern, front_blocks, front_slot, pivot_inverse, update_factor):
    fronts = front_blocks.shape[0]
    columns, total_rows = rhs.shape[1:]
    blocks = total_rows // BLOCK
    assert columns == COLS and pivot_inverse.shape[0] == PAIR
    width = pivot_inverse.shape[1]
    slots = PAIR * n
    seps = blocks - 2 * fronts
    f32, i32 = jnp.float32, jnp.int32
    chunk = next(c for c in (16, 8, 4, 2, 1) if seps % c == 0)
    result = pl.pallas_call(
        functools.partial(kernel, n, fronts, blocks, chunk),
        out_shape=pltpu.VMEM((columns * blocks, BLOCK), f32),
        in_specs=[pl.BlockSpec(memory_space=pl.ANY)] * 6,
        out_specs=pl.BlockSpec(memory_space=pltpu.VMEM),
        scratch_shapes=[
            pltpu.VMEM((columns * blocks, BLOCK), f32),
            pltpu.VMEM((PAIR, n, 3, 4, BLOCK), f32),
            pltpu.VMEM((PAIR, n, 3, 4, BLOCK), f32),
            pltpu.VMEM((PAIR, n, 3, 8, BLOCK), f32),
            pltpu.VMEM((3 * slots + seps, 8, BLOCK), f32),
            pltpu.VMEM((slots, 8, BLOCK), f32),
            pltpu.VMEM((2, n, 8, BLOCK), f32),
            pltpu.VMEM((PAIR, width, width), f32),
            pltpu.VMEM((PAIR, width, width), f32),
            pltpu.VMEM((PAIR, 4, width, width), jnp.bfloat16),
            pltpu.VMEM((seps, BLOCK), i32),
            pltpu.VMEM((seps // chunk * slots * 2, chunk, BLOCK), f32),
            pltpu.SMEM((blocks,), i32),
            pltpu.SMEM((4, fronts), i32),
            pltpu.SMEM((fronts,), i32),
            pltpu.SMEM((slots,), i32),
            pltpu.SMEM((fronts,), i32),
            pltpu.SMEM((blocks,), i32),
            pltpu.SMEM((seps,), i32),
            pltpu.SemaphoreType.DMA((6,)),
            pltpu.SemaphoreType.DMA((PAIR,)),
            pltpu.SemaphoreType.DMA((PAIR,)),
            pltpu.SemaphoreType.DMA((PAIR,)),
            pltpu.SemaphoreType.DMA((PAIR,)),
        ],
        compiler_params=pltpu.CompilerParams(collective_id=0, has_side_effects=True),
    )(
        rhs.reshape(columns * blocks, BLOCK),
        pattern.reshape(-1),
        front_blocks.T,
        front_slot,
        pivot_inverse,
        update_factor,
    )
    return result.reshape(1, columns, total_rows)


def solution(mesh):
    return jax.shard_map(
        functools.partial(on_device, mesh.shape["rows"]),
        mesh=mesh,
        in_specs=(
            P("cols", "rows", None),
            P(None, "cols"),
            P(),
            P(),
            P("rows", None, None),
            P("rows", None, None),
        ),
        out_specs=P("cols", "rows", None),
        check_vma=False,
    )
```

time: 30.8 us -> 23.4 us (0.76)
  Pallas kernels: 29.1 us -> 22.5 us
  local copies, waits for them, and re-layouts: 1.58 us -> 0.66 us
    pallas_call x1, Pallas kernels: 29.1 us -> 22.5 us  [on_device(): pl.pallas_call(functools.partial(kernel, n, fronts, blocks, chunk), out_s...]
    unnamed x1, local copies, waits for them, and re-layouts: 1.58 us -> 0.66 us
where the time goes in v2:
time: 23.4 us; the launch traced here: 23.2 us
  Pallas kernels  22.5 us (96%)
  local copies, waits for them, and re-layouts  0.66 us (3%)
    pallas_call x1, Pallas kernels, on_device(): pl.pallas_call(functools.partial(kernel, n, fronts, blocks, chunk), out_s...  22.5 us
    unnamed x1, local copies, waits for them, and re-layouts  0.66 us

profile of v2, /device:TPU:0, one launch (start us, length us, event | category | flops | bytes accessed | tf_op | source)
XLA Modules:
  0.0 23.2 jit_solution(40690282860636485)
XLA Ops:
  0.0 22.5 %shard_map.64 = f32[288,128]{1,0:T(8,128)S(1)} custom-call(f32[288,128]{1,0:T(8,128)} %bitcast.5, s32[48]{0:T(128)} %bitcast.7, s32[4,16]{1,0:T(4,128)} %bitcast.6, s32[16]{0:T(128)} %slot_hbm.1, f32[2,256,256]{2,1,0:T(8,128)} %inv_hbm.1, f32[2,256,256]{2,1,0:T(8,128)} %upd_hbm.1), custom_call_target="tpu_custom_call" | custom-call | tf_op jit(solution)/shard_map/pallas_call | solution.py:245
  22.5 0.7 %copy.10 = f32[1,6,6144]{2,0,1:T(1,128)} copy(f32[1,6,6144]{2,0,1:T(1,128)S(1)} %bitcast.4) | data formatting | bytes 294912

commit v3 on v2

--- a/solution.py
+++ b/solution.py
@@ -10,6 +10,7 @@
 BLOCK = 128
 COLS = 6
 PAIR = 2
+PARTS = 2
 
 
 def split(value):
@@ -42,17 +43,27 @@
     def target(peer):
         return {"rows": peer, "cols": col}
 
-    order = sorted(range(1, n), key=lambda i: abs(i - n // 2))
-
-    def for_peers(body):
+    half = n // PARTS
+
+    def offset(p):
+        return PARTS * (p % half) + p // half
+
+    def for_part(g, body):
+        first = max(g * half, 1)
         if few:
-            for i in order:
-                body(lax.rem(me + i, n))
+            for p in sorted(range(first, (g + 1) * half), key=lambda p: abs(offset(p) - n // 2)):
+                body(p)
         else:
-            def step(i, carry):
-                body(lax.rem(me + i, n))
+            def step(p, carry):
+                body(p)
                 return carry
-            lax.fori_loop(1, n, step, 0)
+            lax.fori_loop(first, (g + 1) * half, step, 0)
+
+    def ahead(p):
+        return lax.rem(me + offset(p), n)
+
+    def behind(p):
+        return lax.rem(me + n - offset(p), n)
 
     def repeat(count, body, unroll=1):
         def step(i, carry):
@@ -64,13 +75,16 @@
         (rhs_hbm, x), (pattern_hbm, pattern), (fb_hbm, fb), (slot_hbm, slot), (inv_hbm, inv), (upd_hbm, upd),
     ]
     loads = [pltpu.make_async_copy(a, b, local_sem.at[i]) for i, (a, b) in enumerate(pieces)]
-    for i in (3, 2, 1, 0, 4, 5):
+    for i in (3, 2, 1, 0):
         loads[i].start()
 
     barrier = pltpu.get_barrier_semaphore()
-    for_peers(lambda peer: pl.semaphore_signal(
-        barrier, inc=1, device_id=target(peer), device_id_type=pl.DeviceIdType.MESH
-    ))
+    for g in range(PARTS):
+        for_part(g, lambda p: pl.semaphore_signal(
+            barrier, inc=1, device_id=target(ahead(p)), device_id_type=pl.DeviceIdType.MESH
+        ))
+    for i in (4, 5):
+        loads[i].start()
 
     def total(count, term):
         if few:
@@ -94,24 +108,27 @@
         mask = pattern[b].astype(jnp.float32)
         return x[pl.ds(first * blocks + b, count, stride=blocks), :] * mask
 
-    def pack(d):
+    def pack(p):
+        d = ahead(p)
         for k in range(PAIR):
             f = front_of[PAIR * d + k]
             b0, b1 = fb[0, f], fb[1, f]
-            snd[k, d, 0] = block_rows(b0, 0, 4)
-            snd[k, d, 1, 0:2, :] = block_rows(b0, 4, 2)
-            snd[k, d, 1, 2:4, :] = block_rows(b1, 0, 2)
-            snd[k, d, 2] = block_rows(b1, 2, 4)
+            snd[k, p, 0] = block_rows(b0, 0, 4)
+            snd[k, p, 1, 0:2, :] = block_rows(b0, 4, 2)
+            snd[k, p, 1, 2:4, :] = block_rows(b1, 0, 2)
+            snd[k, p, 2] = block_rows(b1, 2, 4)
 
     repeat(n, pack, 2)
     pl.semaphore_wait(barrier, n - 1)
 
+    steps = [(k, g) for k in range(PAIR) for g in range(PARTS)]
+    for i, (k, g) in enumerate(steps):
+        for_part(g, lambda p, i=i, k=k: pltpu.make_async_remote_copy(
+            src_ref=snd.at[k, p], dst_ref=rcv.at[k, p], send_sem=out_send.at[i], recv_sem=out_recv.at[i],
+            device_id=target(ahead(p)), device_id_type=pl.DeviceIdType.MESH,
+        ).start())
     for k in range(PAIR):
-        for_peers(lambda peer, k=k: pltpu.make_async_remote_copy(
-            src_ref=snd.at[k, peer], dst_ref=rcv.at[k, me], send_sem=out_send.at[k], recv_sem=out_recv.at[k],
-            device_id=target(peer), device_id_type=pl.DeviceIdType.MESH,
-        ).start())
-        rcv[k, me] = snd[k, me]
+        rcv[k, 0] = snd[k, 0]
 
     loads[4].wait()
     loads[5].wait()
@@ -125,7 +142,9 @@
 
     def find_place(f):
         s = slot[f]
-        place_of[f] = 3 * (lax.rem(s, PAIR) * n + lax.div(s, PAIR)) + 1
+        away = lax.rem(lax.div(s, PAIR) + n - me, n)
+        p = lax.rem(away, PARTS) * half + lax.div(away, PARTS)
+        place_of[f] = 3 * (lax.rem(s, PAIR) * n + p) + 1
 
     repeat(fronts, find_place, 4)
 
@@ -146,31 +165,36 @@
         return pltpu.make_async_copy(view, view, sem)
 
     def flat(a):
-        return a.reshape(8 * n, BLOCK)
-
-    for k in range(PAIR):
-        landed(rcv.at[k], n - 1, out_recv.at[k]).wait()
-        halves[0, :, 0:4, :] = rcv[k, :, 0]
-        halves[0, :, 4:6, :] = rcv[k, :, 1, 0:2, :]
-        halves[1, :, 0:2, :] = rcv[k, :, 1, 2:4, :]
-        halves[1, :, 2:6, :] = rcv[k, :, 2]
-        pivots = jnp.concatenate([flat(halves[0]), flat(halves[1])], axis=1)
+        return a.reshape(8 * half, BLOCK)
+
+    def remote(g):
+        return half - 1 if g == 0 else half
+
+    for i, (k, g) in enumerate(steps):
+        landed(rcv.at[k], remote(g), out_recv.at[i]).wait()
+        here = slice(g * half, (g + 1) * half)
+        halves[i, 0, :, 0:4, :] = rcv[k, here, 0]
+        halves[i, 0, :, 4:6, :] = rcv[k, here, 1, 0:2, :]
+        halves[i, 1, :, 0:2, :] = rcv[k, here, 1, 2:4, :]
+        halves[i, 1, :, 2:6, :] = rcv[k, here, 2]
+        pivots = jnp.concatenate([flat(halves[i, 0]), flat(halves[i, 1])], axis=1)
         solved = pivots + times_transposed(pivots, wide[k, 0], wide[k, 1])
         update = times_transposed(solved, wide[k, 2], wide[k, 3])
         quads = [
-            half.reshape(n, 8, BLOCK)
-            for half in (solved[:, :BLOCK], solved[:, BLOCK:], update[:, :BLOCK], update[:, BLOCK:])
+            part.reshape(half, 8, BLOCK)
+            for part in (solved[:, :BLOCK], solved[:, BLOCK:], update[:, :BLOCK], update[:, BLOCK:])
         ]
         for t in range(3):
-            back[k, :, t, 0:6, :] = quads[t][:, 0:6]
-            back[k, :, t, 6:8, :] = quads[3][:, 2 * t:2 * t + 2]
-
-        for_peers(lambda peer, k=k: pltpu.make_async_remote_copy(
-            src_ref=back.at[k, peer], dst_ref=pool.at[pl.ds(3 * (k * n + me), 3)],
-            send_sem=back_send.at[k], recv_sem=back_recv.at[k],
-            device_id=target(peer), device_id_type=pl.DeviceIdType.MESH,
+            back[k, here, t, 0:6, :] = quads[t][:, 0:6]
+            back[k, here, t, 6:8, :] = quads[3][:, 2 * t:2 * t + 2]
+
+        for_part(g, lambda p, i=i, k=k: pltpu.make_async_remote_copy(
+            src_ref=back.at[k, p], dst_ref=pool.at[pl.ds(3 * (k * n + p), 3)],
+            send_sem=back_send.at[i], recv_sem=back_recv.at[i],
+            device_id=target(behind(p)), device_id_type=pl.DeviceIdType.MESH,
         ).start())
-        pool[pl.ds(3 * (k * n + me), 3)] = back[k, me]
+        if g == 0:
+            pool[3 * k * n:3 * k * n + 3] = back[k, 0]
 
     def find_separator(j):
         b = lax.fori_loop(
@@ -187,28 +211,30 @@
     def weigh(g):
         rows = sep_rows[pl.ds(pl.multiple_of(g * chunk, chunk), chunk), :]
 
-        def one_slot(s):
-            f = front_of[s]
-            used = slot[f] == s
-            q = lax.rem(s, PAIR) * n + lax.div(s, PAIR)
-            for h in range(2):
-                named = jnp.where(used, fb[2 + h, f], -1)
-                coef[(g * slots + q) * 2 + h] = jnp.where(rows == named, -1.0, 0.0)
-
-        repeat(slots, one_slot, 4)
+        def one_place(p):
+            for k in range(PAIR):
+                s = PAIR * ahead(p) + k
+                f = front_of[s]
+                used = slot[f] == s
+                for h in range(2):
+                    named = jnp.where(used, fb[2 + h, f], -1)
+                    coef[(g * slots + k * n + p) * 2 + h] = jnp.where(rows == named, -1.0, 0.0)
+
+        repeat(n, one_place, 4)
 
     repeat(seps // chunk, weigh)
 
-    for k in range(PAIR):
-        landed(pool, 3 * (n - 1), back_recv.at[k]).wait()
+    for i, (k, part) in enumerate(steps):
+        landed(pool, 3 * remote(part), back_recv.at[i]).wait()
+        begin = k * n + part * half
         for t in range(3):
-            last[k * n:(k + 1) * n, 2 * t:2 * t + 2, :] = pool[pl.ds(3 * k * n + t, n, stride=3), 6:8, :]
-
-        def add_up(g, k=k):
+            last[begin:begin + half, 2 * t:2 * t + 2, :] = pool[pl.ds(3 * begin + t, half, stride=3), 6:8, :]
+
+        def add_up(g, begin=begin):
             first = 3 * slots + g * chunk
 
             def one_slot(o, accs):
-                q = k * n + o
+                q = begin + o
                 parts = (pool[3 * q + 2], last[q])
                 for h in range(2):
                     row = (g * slots + q) * 2 + h
@@ -216,7 +242,7 @@
                 return accs
 
             accs = tuple(pool[first + j] for j in range(chunk))
-            accs = lax.fori_loop(0, n, one_slot, accs, unroll=4 if few else 1)
+            accs = lax.fori_loop(0, half, one_slot, accs, unroll=4 if few else 1)
             for j in range(chunk):
                 pool[first + j] = accs[j]
 
@@ -227,9 +253,9 @@
 
     repeat(blocks, put, 16)
 
-    for k in range(PAIR):
-        landed(snd.at[k], n - 1, out_send.at[k]).wait()
-        landed(back.at[k], n - 1, back_send.at[k]).wait()
+    for i, (k, g) in enumerate(steps):
+        landed(snd.at[k], remote(g), out_send.at[i]).wait()
+        landed(back.at[k], remote(g), back_send.at[i]).wait()
 
 
 def on_device(n, rhs, pattern, front_blocks, front_slot, pivot_inverse, update_factor):
@@ -254,7 +280,7 @@
             pltpu.VMEM((PAIR, n, 3, 8, BLOCK), f32),
             pltpu.VMEM((3 * slots + seps, 8, BLOCK), f32),
             pltpu.VMEM((slots, 8, BLOCK), f32),
-            pltpu.VMEM((2, n, 8, BLOCK), f32),
+            pltpu.VMEM((PAIR * PARTS, 2, n // PARTS, 8, BLOCK), f32),
             pltpu.VMEM((PAIR, width, width), f32),
             pltpu.VMEM((PAIR, width, width), f32),
             pltpu.VMEM((PAIR, 4, width, width), jnp.bfloat16),
@@ -268,10 +294,10 @@
             pltpu.SMEM((blocks,), i32),
             pltpu.SMEM((seps,), i32),
             pltpu.SemaphoreType.DMA((6,)),
-            pltpu.SemaphoreType.DMA((PAIR,)),
-            pltpu.SemaphoreType.DMA((PAIR,)),
-            pltpu.SemaphoreType.DMA((PAIR,)),
-            pltpu.SemaphoreType.DMA((PAIR,)),
+            pltpu.SemaphoreType.DMA((PAIR * PARTS,)),
+            pltpu.SemaphoreType.DMA((PAIR * PARTS,)),
+            pltpu.SemaphoreType.DMA((PAIR * PARTS,)),
+            pltpu.SemaphoreType.DMA((PAIR * PARTS,)),
         ],
         compiler_params=pltpu.CompilerParams(collective_id=0, has_side_effects=True),
     )(

time: 23.4 us -> 23 us (0.983)
  Pallas kernels: 22.5 us -> 22.2 us
    pallas_call x1, Pallas kernels: 22.5 us -> 22.2 us  [on_device(): pl.pallas_call(functools.partial(kernel, n, fronts, blocks, chunk), out_s...]
where the time goes in v3:
time: 23 us; the launch traced here: 22.9 us
  Pallas kernels  22.2 us (97%)
  local copies, waits for them, and re-layouts  0.66 us (3%)
    pallas_call x1, Pallas kernels, on_device(): pl.pallas_call(functools.partial(kernel, n, fronts, blocks, chunk), out_s...  22.2 us
    unnamed x1, local copies, waits for them, and re-layouts  0.66 us

profile of v3, /device:TPU:0, one launch (start us, length us, event | category | flops | bytes accessed | tf_op | source)
XLA Modules:
  0.0 22.9 jit_solution(4542042133207435139)
XLA Ops:
  0.0 22.2 %shard_map.64 = f32[288,128]{1,0:T(8,128)S(1)} custom-call(f32[288,128]{1,0:T(8,128)} %bitcast.5, s32[48]{0:T(128)} %bitcast.7, s32[4,16]{1,0:T(4,128)} %bitcast.6, s32[16]{0:T(128)} %slot_hbm.1, f32[2,256,256]{2,1,0:T(8,128)} %inv_hbm.1, f32[2,256,256]{2,1,0:T(8,128)} %upd_hbm.1), custom_call_target="tpu_custom_call" | custom-call | tf_op jit(solution)/shard_map/pallas_call | solution.py:271
  22.2 0.7 %copy.10 = f32[1,6,6144]{2,0,1:T(1,128)} copy(f32[1,6,6144]{2,0,1:T(1,128)S(1)} %bitcast.4) | data formatting | bytes 294912

commit v4 on v3

--- a/solution.py
+++ b/solution.py
@@ -10,7 +10,7 @@
 BLOCK = 128
 COLS = 6
 PAIR = 2
-PARTS = 2
+PARTS = 4
 
 
 def split(value):

time: 23 us -> 22.4 us (0.974)
  Pallas kernels: 22.2 us -> 21.6 us
    pallas_call x1, Pallas kernels: 22.2 us -> 21.6 us  [on_device(): pl.pallas_call(functools.partial(kernel, n, fronts, blocks, chunk), out_s...]
where the time goes in v4:
time: 22.4 us; the launch traced here: 22.3 us
  Pallas kernels  21.6 us (96%)
  local copies, waits for them, and re-layouts  0.66 us (3%)
    pallas_call x1, Pallas kernels, on_device(): pl.pallas_call(functools.partial(kernel, n, fronts, blocks, chunk), out_s...  21.6 us
    unnamed x1, local copies, waits for them, and re-layouts  0.66 us

profile of v4, /device:TPU:0, one launch (start us, length us, event | category | flops | bytes accessed | tf_op | source)
XLA Modules:
  0.0 22.3 jit_solution(13431709339283816288)
XLA Ops:
  0.0 21.6 %shard_map.64 = f32[288,128]{1,0:T(8,128)S(1)} custom-call(f32[288,128]{1,0:T(8,128)} %bitcast.5, s32[48]{0:T(128)} %bitcast.7, s32[4,16]{1,0:T(4,128)} %bitcast.6, s32[16]{0:T(128)} %slot_hbm.1, f32[2,256,256]{2,1,0:T(8,128)} %inv_hbm.1, f32[2,256,256]{2,1,0:T(8,128)} %upd_hbm.1), custom_call_target="tpu_custom_call" | custom-call | tf_op jit(solution)/shard_map/pallas_call | solution.py:271
  21.6 0.7 %copy.10 = f32[1,6,6144]{2,0,1:T(1,128)} copy(f32[1,6,6144]{2,0,1:T(1,128)S(1)} %bitcast.4) | data formatting | bytes 294912

commit v5 on v4

--- a/solution.py
+++ b/solution.py
@@ -19,8 +19,8 @@
     return high, low
 
 
-def times_transposed(x, high, low):
-    dims = (((1,), (1,)), ((), ()))
+def times(x, high, low, inner):
+    dims = (((1,), (inner,)), ((), ()))
     x_high, x_low = split(x)
     dot = functools.partial(lax.dot_general, dimension_numbers=dims, preferred_element_type=jnp.float32)
     return dot(x_high, high) + (dot(x_low, high) + dot(x_high, low))
@@ -51,7 +51,7 @@
     def for_part(g, body):
         first = max(g * half, 1)
         if few:
-            for p in sorted(range(first, (g + 1) * half), key=lambda p: abs(offset(p) - n // 2)):
+            for p in sorted(range(first, (g + 1) * half), key=lambda p: -abs(offset(p) - n // 2)):
                 body(p)
         else:
             def step(p, carry):
@@ -135,8 +135,9 @@
     width = inv.shape[1]
     strict = lax.broadcasted_iota(jnp.int32, (width, width), 0) > lax.broadcasted_iota(jnp.int32, (width, width), 1)
     for k in range(PAIR):
-        wide[k, 0], wide[k, 1] = split(jnp.where(strict, inv[k], 0.0))
-        wide[k, 2], wide[k, 3] = split(upd[k])
+        high, low = split(jnp.where(strict, inv[k], 0.0))
+        wide[k, 0, :width], wide[k, 1, :width] = high, low
+        wide[k, 0, width:], wide[k, 1, width:] = split(upd[k] + times(upd[k], high, low, 0))
     halves[...] = jnp.zeros(halves.shape, jnp.float32)
     last[...] = jnp.zeros(last.shape, jnp.float32)
 
@@ -178,8 +179,9 @@
         halves[i, 1, :, 0:2, :] = rcv[k, here, 1, 2:4, :]
         halves[i, 1, :, 2:6, :] = rcv[k, here, 2]
         pivots = jnp.concatenate([flat(halves[i, 0]), flat(halves[i, 1])], axis=1)
-        solved = pivots + times_transposed(pivots, wide[k, 0], wide[k, 1])
-        update = times_transposed(solved, wide[k, 2], wide[k, 3])
+        both = times(pivots, wide[k, 0], wide[k, 1], 1)
+        solved = pivots + both[:, :width]
+        update = both[:, width:]
         quads = [
             part.reshape(half, 8, BLOCK)
             for part in (solved[:, :BLOCK], solved[:, BLOCK:], update[:, :BLOCK], update[:, BLOCK:])
@@ -283,7 +285,7 @@
             pltpu.VMEM((PAIR * PARTS, 2, n // PARTS, 8, BLOCK), f32),
             pltpu.VMEM((PAIR, width, width), f32),
             pltpu.VMEM((PAIR, width, width), f32),
-            pltpu.VMEM((PAIR, 4, width, width), jnp.bfloat16),
+            pltpu.VMEM((PAIR, 2, 2 * width, width), jnp.bfloat16),
             pltpu.VMEM((seps, BLOCK), i32),
             pltpu.VMEM((seps // chunk * slots * 2, chunk, BLOCK), f32),
             pltpu.SMEM((blocks,), i32),

time: 22.4 us -> 22.2 us (level)
  no operation moved by 1% of the time
where the time goes in v5:
time: 22.2 us; the launch traced here: 22.1 us
  Pallas kernels  21.4 us (96%)
  local copies, waits for them, and re-layouts  0.66 us (3%)
    pallas_call x1, Pallas kernels, on_device(): pl.pallas_call(functools.partial(kernel, n, fronts, blocks, chunk), out_s...  21.4 us
    unnamed x1, local copies, waits for them, and re-layouts  0.66 us

profile of v5, /device:TPU:0, one launch (start us, length us, event | category | flops | bytes accessed | tf_op | source)
XLA Modules:
  0.0 22.1 jit_solution(5296935114692283299)
XLA Ops:
  0.0 21.4 %shard_map.64 = f32[288,128]{1,0:T(8,128)S(1)} custom-call(f32[288,128]{1,0:T(8,128)} %bitcast.5, s32[48]{0:T(128)} %bitcast.7, s32[4,16]{1,0:T(4,128)} %bitcast.6, s32[16]{0:T(128)} %slot_hbm.1, f32[2,256,256]{2,1,0:T(8,128)} %inv_hbm.1, f32[2,256,256]{2,1,0:T(8,128)} %upd_hbm.1), custom_call_target="tpu_custom_call" | custom-call | tf_op jit(solution)/shard_map/pallas_call | solution.py:273
  21.4 0.7 %copy.10 = f32[1,6,6144]{2,0,1:T(1,128)} copy(f32[1,6,6144]{2,0,1:T(1,128)S(1)} %bitcast.4) | data formatting | bytes 294912

commit v6 on v5

--- a/solution.py
+++ b/solution.py
@@ -10,7 +10,7 @@
 BLOCK = 128
 COLS = 6
 PAIR = 2
-PARTS = 4
+PARTS = 8
 
 
 def split(value):
@@ -121,7 +121,7 @@
     repeat(n, pack, 2)
     pl.semaphore_wait(barrier, n - 1)
 
-    steps = [(k, g) for k in range(PAIR) for g in range(PARTS)]
+    steps = [(k, g) for g in range(PARTS) for k in range(PAIR)]
     for i, (k, g) in enumerate(steps):
         for_part(g, lambda p, i=i, k=k: pltpu.make_async_remote_copy(
             src_ref=snd.at[k, p], dst_ref=rcv.at[k, p], send_sem=out_send.at[i], recv_sem=out_recv.at[i],

time: 22.2 us -> 21.8 us (0.982)
  Pallas kernels: 21.4 us -> 21 us
    pallas_call x1, Pallas kernels: 21.4 us -> 21 us  [on_device(): pl.pallas_call(functools.partial(kernel, n, fronts, blocks, chunk), out_s...]
where the time goes in v6:
time: 21.8 us; the launch traced here: 21.7 us
  Pallas kernels  21 us (96%)
  local copies, waits for them, and re-layouts  0.66 us (3%)
    pallas_call x1, Pallas kernels, on_device(): pl.pallas_call(functools.partial(kernel, n, fronts, blocks, chunk), out_s...  21 us
    unnamed x1, local copies, waits for them, and re-layouts  0.66 us

profile of v6, /device:TPU:0, one launch (start us, length us, event | category | flops | bytes accessed | tf_op | source)
XLA Modules:
  0.0 21.7 jit_solution(2793007568326498553)
XLA Ops:
  0.0 21.0 %shard_map.64 = f32[288,128]{1,0:T(8,128)S(1)} custom-call(f32[288,128]{1,0:T(8,128)} %bitcast.5, s32[48]{0:T(128)} %bitcast.7, s32[4,16]{1,0:T(4,128)} %bitcast.6, s32[16]{0:T(128)} %slot_hbm.1, f32[2,256,256]{2,1,0:T(8,128)} %inv_hbm.1, f32[2,256,256]{2,1,0:T(8,128)} %upd_hbm.1), custom_call_target="tpu_custom_call" | custom-call | tf_op jit(solution)/shard_map/pallas_call | solution.py:273
  21.0 0.7 %copy.10 = f32[1,6,6144]{2,0,1:T(1,128)} copy(f32[1,6,6144]{2,0,1:T(1,128)S(1)} %bitcast.4) | data formatting | bytes 294912
